TPU v7x, 32 devices: a whole 2x2x4 slice. The times are simulated.
32 devices in a mesh: attn: 4 (over y, x), expert: 8 (over z, core).
Axes of the slice: x: 2, y: 2, z: 4, core: 2. Of those that a mesh axis runs over, the one named last changes fastest.
Arguments:
- tokens: bfloat16 [1024, 2880], P(('attn', 'expert')), may hold values from -6 to 6
- expert_ids: int32 [1024, 4], P(('attn', 'expert')), may hold values from 0 to 7, all different within a row; in each aligned block of 32 rows (0 to 31, 32 to 63, ...) at most 32 rows name the same one
- gate_probs: float32 [1024, 4], P(('attn', 'expert')), may hold values from 0.05 to 0.6
- shed_blocks: int32 [8], replicated, may hold values from 0 to 4, as said below
- partner: int32 [8], replicated, may hold values from 0 to 7, as said below
- gate_weight: bfloat16 [8, 2880, 2880], P('expert', None, 'attn'), may hold values from -0.109375 to 0.109375
- up_weight: bfloat16 [8, 2880, 2880], P('expert', None, 'attn'), may hold values from -0.109375 to 0.109375
- down_weight: bfloat16 [8, 2880, 2880], P('expert', 'attn'), may hold values from -0.109375 to 0.109375
Outputs:
- moe_out: bfloat16 [1024, 2880], P(('attn', 'expert'))
Inputs may be any that keep to these rules, and one draw needn't show every extreme that they name: `expert_ids`: in the rows of one device, no expert is named by more than 32 rows; the 4 experts of a token differ. `shed_blocks`: some expert has exactly 4. partner pairs the experts: partner[partner[e]] = e and partner[e] != e.
All inputs are finite; a program needn't handle non-finite values.
Results may differ from a plain program's by a relative error of at most 0.0081.
Values may be sent and summed in bfloat16 or wider, within the bound.
A program may use at most 128 MiB of HBM per device.

v0:
```python
import jax
import jax.numpy as jnp
from jax import lax
from jax.sharding import PartitionSpec as P

SHED_MOST = 4
SWISH_SCALE = 1.702


def lookup(table, indices):
    places = jnp.arange(table.shape[0], dtype=jnp.int32)
    return jnp.sum(jnp.where(indices[:, None] == places[None, :], table[None, :], 0), axis=1)


def activate(rows, gate_w, up_w):
    gate_part = jnp.dot(rows, gate_w, preferred_element_type=jnp.float32)
    up_part = jnp.dot(rows, up_w, preferred_element_type=jnp.float32)
    return (gate_part * jax.nn.sigmoid(SWISH_SCALE * gate_part) * (up_part + 1.0)).astype(
        jnp.bfloat16
    )


def on_device(
    tokens, expert_ids, gate_probs, shed_blocks, partner, gate_weight, up_weight, down_weight
):
    tok_rows, model_width = tokens.shape
    top_count = expert_ids.shape[1]
    expert_count = shed_blocks.shape[0]
    group_count = lax.axis_size("attn")
    capacity = tok_rows * top_count * group_count
    block_size = capacity // 8
    most_rows = min(tok_rows, 3 * tok_rows * top_count // expert_count)
    slot_count = 2 * most_rows
    places = jnp.arange(expert_count, dtype=jnp.int32)
    flat_ids = expert_ids.reshape(-1)
    onehot = (flat_ids[:, None] == places[None, :]).astype(jnp.int32)
    counts = jnp.sum(onehot, axis=0)
    local_rank = jnp.sum((jnp.cumsum(onehot, axis=0) - onehot) * onehot, axis=1)
    everyone = lax.all_gather(counts[None, :], ("attn", "expert"), axis=0, tiled=True)
    position_now = lax.axis_index(("attn", "expert"))
    earlier = (jnp.arange(everyone.shape[0], dtype=jnp.int32) < position_now)[:, None]
    offsets = jnp.sum(jnp.where(earlier, everyone, 0), axis=0)
    global_rank = local_rank + jnp.sum(onehot * offsets[None, :], axis=1)
    limit = capacity - block_size * lookup(shed_blocks, partner)
    own_limit = lookup(limit, flat_ids)
    own_shed = lookup(shed_blocks, flat_ids)
    native = global_rank < own_limit
    borrowed = jnp.logical_and(
        jnp.logical_not(native), global_rank < own_limit + block_size * own_shed
    )
    usable = jnp.logical_or(native, borrowed)
    target = jnp.where(usable, flat_ids, -1)
    table_rows = capacity + block_size * SHED_MOST
    target_hot = (target[:, None] == places[None, :]).astype(jnp.int32)
    position = jnp.sum((jnp.cumsum(target_hot, axis=0) - target_hot) * target_hot, axis=1)
    buffer_index = jnp.where(usable, target * slot_count + position, expert_count * slot_count)
    token_rows = jnp.repeat(tokens, top_count, axis=0)
    send_rows = (
        jnp.zeros((expert_count * slot_count, model_width), jnp.bfloat16)
        .at[buffer_index]
        .set(token_rows, mode="drop")
    )
    send_slots = (
        jnp.full((expert_count * slot_count,), table_rows, jnp.int32)
        .at[buffer_index]
        .set(global_rank, mode="drop")
    )
    send_rows = send_rows.reshape(expert_count, slot_count, model_width)
    send_slots = send_slots.reshape(expert_count, slot_count)
    got_rows, got_slots = (
        lax.all_to_all(send_rows, "expert", split_axis=0, concat_axis=0, tiled=True),
        lax.all_to_all(send_slots, "expert", split_axis=0, concat_axis=0, tiled=True),
    )
    local_table = (
        jnp.zeros((table_rows, model_width), jnp.float32)
        .at[got_slots.reshape(-1)]
        .set(got_rows.reshape(-1, model_width).astype(jnp.float32), mode="drop")
    )
    compact = lax.psum(local_table.astype(jnp.bfloat16), "attn")
    gate_own = gate_weight[0]
    up_own = up_weight[0]
    down_own = down_weight[0]
    hidden_own = activate(compact, gate_own, up_own)
    share = lax.psum_scatter(
        jnp.dot(hidden_own, down_own, preferred_element_type=jnp.float32),
        "attn",
        scatter_dimension=0,
        tiled=True,
    )
    results = lax.all_gather(share.astype(jnp.bfloat16), "attn", axis=0, tiled=True)
    answers = results[jnp.minimum(got_slots, table_rows - 1)]
    returned = lax.all_to_all(answers, "expert", split_axis=0, concat_axis=0, tiled=True)
    flat_back = returned.reshape(expert_count * slot_count, model_width)
    picked = flat_back[jnp.minimum(buffer_index, expert_count * slot_count - 1)]
    weights = jnp.where(usable, gate_probs.reshape(-1), 0.0)
    mixed = picked.astype(jnp.float32) * weights[:, None]
    return mixed.reshape(tok_rows, top_count, model_width).sum(axis=1).astype(jnp.bfloat16)


def solution(mesh):
    in_specs = (
        P(("attn", "expert"), None),
        P(("attn", "expert"), None),
        P(("attn", "expert"), None),
        P(),
        P(),
        P("expert", None, "attn"),
        P("expert", None, "attn"),
        P("expert", "attn", None),
    )
    out_specs = P(("attn", "expert"), None)
    return jax.shard_map(
        on_device, mesh=mesh, in_specs=in_specs, out_specs=out_specs, check_vma=False
    )
```

profile of v0, /device:TPU:0, one launch (start us, length us, event | category | flops | bytes accessed | tf_op | source)
XLA Modules:
  0.0 529.1 jit_solution(730793958750302019)
XLA Ops:
  6.5 0.8 copy.15
  7.3 0.1 eq.20
  7.4 0.1 fusion.17
  7.5 0.1 fusion.16
  7.6 0.1 reshape.235
  7.7 0.2 dynamic-update-slice
  8.0 42.0 %all-reduce = s32[256]{0:T(256)S(1)} all-reduce(s32[256]{0:T(256)S(1)} %dynamic-update-slice), channel_id=2, replica_groups=mesh['attn'=4,'expert'=8] {'attn','expert'}, use_global_device_ids=true, to_apply=%add | all-reduce | flops 256 | bytes 2048
  49.9 0.1 reshape.282
  50.0 0.2 reduce_window_sum.17
  50.2 0.9 select_reduce_fusion.6
  51.1 0.1 select_reduce_fusion.5
  51.1 0.9 select_reduce_fusion.1
  52.0 0.1 fusion.15
  52.1 0.2 reduce_window_sum.18
  52.3 0.2 select_reduce_fusion
  52.5 1.0 scatter_custom_fusion
  53.5 0.7 all_to_all.12
  54.2 3.6 all-to-all-start
  57.8 1.1 broadcast_in_dim.95
  58.9 0.4 reshape.270
  59.3 3.8 scatter_custom_fusion.1
  63.0 0.2 all-to-all-done
  63.3 4.9 all-to-all-start.1
  68.2 0.5 broadcast.220
  68.7 0.7 broadcast_minimum_fusion
  69.4 0.1 reshape.236
  69.5 67.4 %all-to-all-done.1 = bf16[8,64,2880]{2,1,0:T(8,128)(2,1)S(1)} async-done(((bf16[8,64,2880]{2,1,0:T(8,128)(2,1)}), bf16[8,64,2880]{2,1,0:T(8,128)(2,1)S(1)}, u32[]{:S(2)}, u32[]{:S(2)}) %all-to-all-start.1) | async-done | bytes 2949152 | tf_op jit(solution)/shard_map/all_to_all | solution.py:71
  136.8 8.4 %scatter_custom_fusion.2 = f32[768,2880]{1,0:T(8,128)} fusion(s32[512]{0:T(512)S(1)} %bitcast.54, bf16[512,2880]{1,0:T(8,128)(2,1)S(1)} %bitcast.51, f32[]{:T(128)} %constant.14.clone.1), kind=kCustom, calls=%fused_computation.5 | custom fusion | flops 1474560 | bytes 11862020 | tf_op jit(solution)/shard_map/scatter | solution.py:77
  145.3 6.1 %convert_element_type.35 = bf16[768,2880]{1,0:T(8,128)(2,1)} convert(f32[768,2880]{1,0:T(8,128)} %scatter_custom_fusion.2) | non-fusion elementwise | flops 2211840 | bytes 13271040 | tf_op jit(solution)/shard_map/convert_element_type | solution.py:79
  151.4 0.2 reduce-scatter.2.cloned.1.call-start
  151.6 107.7 %all-reduce.3.cloned.1.call-done = bf16[768,2880]{1,0:T(8,128)(2,1)} async-done(((bf16[768,2880]{1,0:T(8,128)(2,1)}), bf16[768,2880]{1,0:T(8,128)(2,1)}) %all-reduce.3.cloned.1.call-update) | async-done | bytes 4423696 | tf_op jit(solution)/shard_map/psum | solution.py:79
  259.3 6.8 %fusion.5 = f32[768,720]{0,1:T(8,128)S(1)} fusion(bf16[768,2880]{1,0:T(8,128)(2,1)} %all-reduce.3.cloned.1.call-done, bf16[1,2880,720]{1,2,0:T(8,128)(2,1)} %param.14), kind=kOutput, calls=%fused_computation.10 | convolution fusion | flops 3185049600 | bytes 10782720 | tf_op jit(solution)/shard_map/dot_general | solution.py:17
  266.1 18.0 %fusion.3 = f32[768,2880]{1,0:T(8,128)} fusion(bf16[1,720,2880]{2,1,0:T(8,128)(2,1)} %param.15, f32[768,720]{0,1:T(8,128)S(1)} %fusion.5, bf16[768,2880]{1,0:T(8,128)(2,1)} %all-reduce.3.cloned.1.call-done, bf16[1,2880,720]{1,2,0:T(8,128)(2,1)} %param.13), kind=kOutput, calls=%fused_computation.8 | convolution fusion | flops 6374522880 | bytes 23777280 | tf_op jit(solution)/shard_map/dot_general | solution.py:85
  284.1 0.3 all-gather.3.cloned.1.call-start
  284.4 91.6 %reduce-scatter.2.cloned.1.call-done = f32[192,2880]{1,0:T(8,128)} async-done(((f32[768,2880]{1,0:T(8,128)}), f32[192,2880]{1,0:T(8,128)}) %reduce-scatter.2.cloned.1.call-update) | async-done | bytes 2211856 | tf_op jit(solution)/shard_map/reduce_scatter | solution.py:84
  376.0 2.8 convert_element_type.37
  378.8 0.1 reshape.244
  378.9 55.4 %all-gather.3.cloned.1.call-done = bf16[768,2880]{1,0:T(8,128)(2,1)} async-done(((bf16[192,2880]{1,0:T(8,128)(2,1)}), bf16[768,2880]{1,0:T(8,128)(2,1)}) %all-gather.3.cloned.1.call-update) | async-done | bytes 4423696 | tf_op jit(solution)/shard_map/all_gather | solution.py:90
  434.2 9.6 %gather_fusion = bf16[512,2880]{1,0:T(8,128)(2,1)} fusion(bf16[768,2880]{1,0:T(8,128)(2,1)} %all-gather.3.cloned.1.call-done, s32[1024]{0:T(1024)S(1)} %pad_clamp_fusion.1), kind=kCustom, calls=%fused_computation | custom fusion | bytes 5900288 | tf_op jit(solution)/shard_map/gather | solution.py:91
  443.8 4.7 all-to-all-start.2
  448.6 0.1 add.134
  448.7 0.1 reduce_sum.97
  448.8 0.1 mul.98
  448.9 0.1 copy.17
  449.0 68.3 %all-to-all-done.2 = bf16[8,64,2880]{2,1,0:T(8,128)(2,1)S(1)} async-done(((bf16[8,64,2880]{2,1,0:T(8,128)(2,1)}), bf16[8,64,2880]{2,1,0:T(8,128)(2,1)S(1)}, u32[]{:S(2)}, u32[]{:S(2)}) %all-to-all-start.2) | async-done | bytes 2949152 | tf_op jit(solution)/shard_map/all_to_all | solution.py:92
  517.3 1.9 gather_fusion.1
  519.2 1.7 reshape.241
  520.8 1.7 multiply_reduce_fusion
  (17 shorter events, 0.2 us)
Async XLA Ops:
  54.2 9.1 %all-to-all-start = ((s32[8,1,64]{2,1,0:T(1,128)}), s32[8,1,64]{2,1,0:T(1,128)S(1)}, u32[]{:S(2)}, u32[]{:S(2)}) async-start(s32[8,1,64]{2,1,0:T(1,128)} %all_to_all.12), calls=%async_computation | async-start | bytes 8192 | tf_op jit(solution)/shard_map/all_to_all | solution.py:72
  63.3 73.6 %all-to-all-start.1 = ((bf16[8,64,2880]{2,1,0:T(8,128)(2,1)}), bf16[8,64,2880]{2,1,0:T(8,128)(2,1)S(1)}, u32[]{:S(2)}, u32[]{:S(2)}) async-start(bf16[8,64,2880]{2,1,0:T(8,128)(2,1)} %bitcast.6), calls=%async_computation.1 | async-start | bytes 6029312 | tf_op jit(solution)/shard_map/all_to_all | solution.py:71
  68.2 191.2 %all-reduce.3.cloned.1.call-start = ((), (), s32[]{:S(2)}) async-start(), calls=%async_computation.4 | async-start | bytes 9043968 | tf_op jit(solution)/shard_map/psum | solution.py:79
  151.4 224.6 %reduce-scatter.2.cloned.1.call-start = ((), (), s32[]{:S(2)}) async-start(), calls=%async_computation.5 | async-start | bytes 11304960 | tf_op jit(solution)/shard_map/reduce_scatter | solution.py:84
  284.1 150.1 %all-gather.3.cloned.1.call-start = ((), (), s32[]{:S(2)}) async-start(), calls=%async_computation.6 | async-start | bytes 5652480 | tf_op jit(solution)/shard_map/all_gather | solution.py:90
  443.8 5.1 copy-start
  443.8 73.4 %all-to-all-start.2 = ((bf16[8,64,2880]{2,1,0:T(8,128)(2,1)}), bf16[8,64,2880]{2,1,0:T(8,128)(2,1)S(1)}, u32[]{:S(2)}, u32[]{:S(2)}) async-start(bf16[8,64,2880]{2,1,0:T(8,128)(2,1)} %bitcast.52), calls=%async_computation.3 | async-start | bytes 6029312 | tf_op jit(solution)/shard_map/all_to_all | solution.py:92
Sparse Core Ops, SparseCore 0:
  151.5 107.7 all-reduce.2
  284.3 91.6 reduce-scatter.1
  378.9 55.2 all-gather.2
where the time goes:
time: 530 us; the launch traced here: 529 us
  waiting for transfers between devices  391 us (74%)
  blocking collectives  42 us (8%)
  matrix products  24.8 us (5%)
  local copies, waits for them, and re-layouts  22.4 us (4%)
  other arithmetic  22.3 us (4%)
  starting transfers between devices  13.7 us (3%)
  between operations  13.3 us (3%)
    psum x1, waiting for transfers between devices, on_device(): compact = lax.psum(local_table.astype(jnp.bfloat16), 'attn')  108 us
    reduce_scatter x1, waiting for transfers between devices, on_device(): lax.psum_scatter(jnp.dot(hidden_own, down_own, preferred_element_type=jnp...  91.6 us
    all_to_all x1, waiting for transfers between devices, on_device(): lax.all_to_all(answers, 'expert', split_axis=0, concat_axis=0, tiled=True)  68.3 us
    all_to_all x1, waiting for transfers between devices, on_device(): lax.all_to_all(send_rows, 'expert', split_axis=0, concat_axis=0, tiled=True)  67.4 us
    all_gather x1, waiting for transfers between devices, on_device(): lax.all_gather(share.astype(jnp.bfloat16), 'attn', axis=0, tiled=True)  55.4 us
    unnamed x1, blocking collectives  42 us
    dot_general x1, matrix products, on_device(): jnp.dot(hidden_own, down_own, preferred_element_type=jnp.float32)  18 us
  transfers between devices with their start and end apart: 6, of which 6 were waited for; matrix products, arithmetic and copies ran while one was open for 1% of the time, Pallas kernels for 0%

commit v1 on v0

--- a/solution.py
+++ b/solution.py
@@ -5,6 +5,11 @@
 
 SHED_MOST = 4
 SWISH_SCALE = 1.702
+
+
+def add_all(x, axis):
+    parts = lax.all_gather(x, axis)
+    return jnp.sum(parts, axis=0)
 
 
 def lookup(table, indices):
@@ -76,7 +81,7 @@
         .at[got_slots.reshape(-1)]
         .set(got_rows.reshape(-1, model_width).astype(jnp.float32), mode="drop")
     )
-    compact = lax.psum(local_table.astype(jnp.bfloat16), "attn")
+    compact = add_all(local_table.astype(jnp.bfloat16), "attn")
     gate_own = gate_weight[0]
     up_own = up_weight[0]
     down_own = down_weight[0]

time: 530 us -> 602 us (1.14)
  waiting for transfers between devices: 391 us -> 451 us
  other arithmetic: 22.3 us -> 34.7 us
    all_gather x0 -> x1, waiting for transfers between devices: none -> 168 us  [add_all(): parts = lax.all_gather(x, axis)]
    psum x1 -> x0, waiting for transfers between devices: 108 us -> none  [on_device(): compact = lax.psum(local_table.astype(jnp.bfloat16), 'attn')]
    unnamed x0 -> x1, other arithmetic: none -> 12.4 us
where the time goes in v1:
time: 602 us
  waiting for transfers between devices  451 us (75%)
  blocking collectives  42 us (7%)
  other arithmetic  34.7 us (6%)
  matrix products  24.8 us (4%)
  local copies, waits for them, and re-layouts  22.4 us (4%)
  starting transfers between devices  13.7 us (2%)
  between operations  13.3 us (2%)
    all_gather x1, waiting for transfers between devices, add_all(): parts = lax.all_gather(x, axis)  168 us
    reduce_scatter x1, waiting for transfers between devices, on_device(): lax.psum_scatter(jnp.dot(hidden_own, down_own, preferred_element_type=jnp...  91.6 us
    all_to_all x1, waiting for transfers between devices, on_device(): lax.all_to_all(answers, 'expert', split_axis=0, concat_axis=0, tiled=True)  68.3 us
    all_to_all x1, waiting for transfers between devices, on_device(): lax.all_to_all(send_rows, 'expert', split_axis=0, concat_axis=0, tiled=True)  67.4 us
    all_gather x1, waiting for transfers between devices, on_device(): lax.all_gather(share.astype(jnp.bfloat16), 'attn', axis=0, tiled=True)  55.4 us
    unnamed x1, blocking collectives  42 us
    dot_general x1, matrix products, on_device(): jnp.dot(hidden_own, down_own, preferred_element_type=jnp.float32)  18 us
    unnamed x1, other arithmetic  12.4 us
  transfers between devices with their start and end apart: 6, of which 6 were waited for; matrix products, arithmetic and copies ran while one was open for 1% of the time, Pallas kernels for 0%

profile of v1, /device:TPU:0, one launch (start us, length us, event | category | flops | bytes accessed | tf_op | source)
XLA Modules:
  0.0 601.8 jit_solution(9270770664053945203)
XLA Ops:
  6.5 0.8 copy.18
  7.3 0.1 eq.20
  7.4 0.1 fusion.17
  7.5 0.1 fusion.16
  7.6 0.1 reshape.235
  7.7 0.2 dynamic-update-slice
  8.0 42.0 %all-reduce = s32[256]{0:T(256)S(1)} all-reduce(s32[256]{0:T(256)S(1)} %dynamic-update-slice), channel_id=2, replica_groups=mesh['attn'=4,'expert'=8] {'attn','expert'}, use_global_device_ids=true, to_apply=%add | all-reduce | flops 256 | bytes 2048
  49.9 0.1 reshape.282
  50.0 0.2 reduce_window_sum.17
  50.2 0.9 select_reduce_fusion.6
  51.1 0.1 select_reduce_fusion.5
  51.2 0.9 select_reduce_fusion.1
  52.0 0.1 fusion.15
  52.1 0.2 reduce_window_sum.18
  52.3 0.2 select_reduce_fusion
  52.5 1.0 scatter_custom_fusion
  53.5 0.7 all_to_all.12
  54.2 3.6 all-to-all-start
  57.8 1.1 broadcast_in_dim.95
  58.9 0.4 reshape.270
  59.3 3.8 scatter_custom_fusion.1
  63.1 0.2 all-to-all-done
  63.3 4.9 all-to-all-start.1
  68.2 0.5 broadcast.220
  68.7 0.7 broadcast_minimum_fusion
  69.4 0.1 reshape.236
  69.5 67.4 %all-to-all-done.1 = bf16[8,64,2880]{2,1,0:T(8,128)(2,1)S(1)} async-done(((bf16[8,64,2880]{2,1,0:T(8,128)(2,1)}), bf16[8,64,2880]{2,1,0:T(8,128)(2,1)S(1)}, u32[]{:S(2)}, u32[]{:S(2)}) %all-to-all-start.1) | async-done | bytes 2949152 | tf_op jit(solution)/shard_map/all_to_all | solution.py:76
  136.8 8.4 %scatter_custom_fusion.2 = f32[768,2880]{1,0:T(8,128)} fusion(s32[512]{0:T(512)S(1)} %bitcast.56, bf16[512,2880]{1,0:T(8,128)(2,1)S(1)} %bitcast.53, f32[]{:T(128)} %constant.14.clone.1), kind=kCustom, calls=%fused_computation.5 | custom fusion | flops 1474560 | bytes 11862020 | tf_op jit(solution)/shard_map/scatter | solution.py:82
  145.3 6.1 %convert_element_type.37 = bf16[768,2880]{1,0:T(8,128)(2,1)} convert(f32[768,2880]{1,0:T(8,128)} %scatter_custom_fusion.2) | non-fusion elementwise | flops 2211840 | bytes 13271040 | tf_op jit(solution)/shard_map/convert_element_type | solution.py:84
  151.4 0.2 reduce-scatter.2.cloned.1.call-start
  151.7 168.0 %all-gather.7.cloned.1.call-done = bf16[3072,2880]{1,0:T(8,128)(2,1)} async-done(((bf16[768,2880]{1,0:T(8,128)(2,1)}), bf16[3072,2880]{1,0:T(8,128)(2,1)}) %all-gather.7.cloned.1.call-update) | async-done | bytes 17694736 | tf_op jit(solution)/shard_map/all_gather | solution.py:11
  319.7 12.4 %reduce_sum.109 = bf16[768,2880]{1,0:T(8,128)(2,1)} reduce(bf16[4,768,2880]{2,1,0:T(8,128)(2,1)} %bitcast.52, bf16[]{:T(256)} %constant.23.clone.1), dimensions={0}, to_apply=%region_13.14 | reduce | flops 6635520 | bytes 22118402
  332.0 6.8 %fusion.5 = f32[768,720]{0,1:T(8,128)S(1)} fusion(bf16[768,2880]{1,0:T(8,128)(2,1)} %reduce_sum.109, bf16[1,2880,720]{1,2,0:T(8,128)(2,1)} %param.14), kind=kOutput, calls=%fused_computation.10 | convolution fusion | flops 3185049600 | bytes 10782720 | tf_op jit(solution)/shard_map/dot_general | solution.py:22
  338.8 18.0 %fusion.3 = f32[768,2880]{1,0:T(8,128)} fusion(bf16[1,720,2880]{2,1,0:T(8,128)(2,1)} %param.15, f32[768,720]{0,1:T(8,128)S(1)} %fusion.5, bf16[768,2880]{1,0:T(8,128)(2,1)} %reduce_sum.109, bf16[1,2880,720]{1,2,0:T(8,128)(2,1)} %param.13), kind=kOutput, calls=%fused_computation.8 | convolution fusion | flops 6374522880 | bytes 23777280 | tf_op jit(solution)/shard_map/dot_general | solution.py:90
  356.9 0.3 all-gather.5.cloned.1.call-start
  357.1 91.6 %reduce-scatter.2.cloned.1.call-done = f32[192,2880]{1,0:T(8,128)} async-done(((f32[768,2880]{1,0:T(8,128)}), f32[192,2880]{1,0:T(8,128)}) %reduce-scatter.2.cloned.1.call-update) | async-done | bytes 2211856 | tf_op jit(solution)/shard_map/reduce_scatter | solution.py:89
  448.7 2.8 convert_element_type.39
  451.6 55.4 %all-gather.5.cloned.1.call-done = bf16[768,2880]{1,0:T(8,128)(2,1)} async-done(((bf16[192,2880]{1,0:T(8,128)(2,1)}), bf16[768,2880]{1,0:T(8,128)(2,1)}) %all-gather.5.cloned.1.call-update) | async-done | bytes 4423696 | tf_op jit(solution)/shard_map/all_gather | solution.py:95
  507.0 9.6 %gather_fusion = bf16[512,2880]{1,0:T(8,128)(2,1)} fusion(bf16[768,2880]{1,0:T(8,128)(2,1)} %all-gather.5.cloned.1.call-done, s32[1024]{0:T(1024)S(1)} %pad_clamp_fusion.1), kind=kCustom, calls=%fused_computation | custom fusion | bytes 5900288 | tf_op jit(solution)/shard_map/gather | solution.py:96
  516.6 4.7 all-to-all-start.2
  521.3 0.1 add.132
  521.4 0.1 reduce_sum.110
  521.5 0.1 mul.98
  521.7 0.1 copy.21
  521.8 68.3 %all-to-all-done.2 = bf16[8,64,2880]{2,1,0:T(8,128)(2,1)S(1)} async-done(((bf16[8,64,2880]{2,1,0:T(8,128)(2,1)}), bf16[8,64,2880]{2,1,0:T(8,128)(2,1)S(1)}, u32[]{:S(2)}, u32[]{:S(2)}) %all-to-all-start.2) | async-done | bytes 2949152 | tf_op jit(solution)/shard_map/all_to_all | solution.py:97
  590.0 1.9 gather_fusion.1
  591.9 1.7 reshape.241
  593.6 1.7 multiply_reduce_fusion
  (18 shorter events, 0.3 us)
Async XLA Ops:
  54.2 9.1 %all-to-all-start = ((s32[8,1,64]{2,1,0:T(1,128)}), s32[8,1,64]{2,1,0:T(1,128)S(1)}, u32[]{:S(2)}, u32[]{:S(2)}) async-start(s32[8,1,64]{2,1,0:T(1,128)} %all_to_all.12), calls=%async_computation | async-start | bytes 8192 | tf_op jit(solution)/shard_map/all_to_all | solution.py:77
  63.3 73.6 %all-to-all-start.1 = ((bf16[8,64,2880]{2,1,0:T(8,128)(2,1)}), bf16[8,64,2880]{2,1,0:T(8,128)(2,1)S(1)}, u32[]{:S(2)}, u32[]{:S(2)}) async-start(bf16[8,64,2880]{2,1,0:T(8,128)(2,1)} %bitcast.6), calls=%async_computation.1 | async-start | bytes 6029312 | tf_op jit(solution)/shard_map/all_to_all | solution.py:76
  68.2 251.5 %all-gather.7.cloned.1.call-start = ((), (), s32[]{:S(2)}) async-start(), calls=%async_computation.6 | async-start | bytes 22609920 | tf_op jit(solution)/shard_map/all_gather | solution.py:11
  151.4 297.3 %reduce-scatter.2.cloned.1.call-start = ((), (), s32[]{:S(2)}) async-start(), calls=%async_computation.4 | async-start | bytes 11304960 | tf_op jit(solution)/shard_map/reduce_scatter | solution.py:89
  356.9 150.1 %all-gather.5.cloned.1.call-start = ((), (), s32[]{:S(2)}) async-start(), calls=%async_computation.5 | async-start | bytes 5652480 | tf_op jit(solution)/shard_map/all_gather | solution.py:95
  516.6 5.1 copy-start
  516.6 73.4 %all-to-all-start.2 = ((bf16[8,64,2880]{2,1,0:T(8,128)(2,1)}), bf16[8,64,2880]{2,1,0:T(8,128)(2,1)S(1)}, u32[]{:S(2)}, u32[]{:S(2)}) async-start(bf16[8,64,2880]{2,1,0:T(8,128)(2,1)} %bitcast.54), calls=%async_computation.3 | async-start | bytes 6029312 | tf_op jit(solution)/shard_map/all_to_all | solution.py:97
Sparse Core Ops, SparseCore 0:
  151.5 168.0 all-gather.6
  357.0 91.6 reduce-scatter.1
  451.6 55.2 all-gather.4
